TPU v7x, 32 devices: a whole 2x2x4 slice. The times are simulated.
32 devices in a mesh: prompt: 4 (over y, x), resp: 8 (over z, core).
Axes of the slice: x: 2, y: 2, z: 4, core: 2. Of those that a mesh axis runs over, the one named last changes fastest.
Arguments:
- embeddings: bfloat16 [32, 256, 3584], P('prompt', 'resp'), parts along dimension 0, may hold values from -6 to 6
- head_weight: bfloat16 [3584, 3584], P('resp'), may hold values from -0.0017089844 to 0.0017089844
- valid_mask: int32 [32, 256], P('prompt', 'resp'), parts along dimension 0, may hold values from 0 to 1, as said below
Outputs:
- preferences: float32 [32, 256, 256], P('prompt', 'resp'), parts along dimension 0
- win_rates: float32 [32, 256], P('prompt', 'resp'), parts along dimension 0
There are 4 independent parts, one for each index of `prompt`. A program takes and returns all parts, laid end to end along the dimension named above; an argument that names none is the same for every part. Nothing has to cross between parts.
Inputs may be any that keep to these rules, and one draw needn't show every extreme that they name: `valid_mask`: for each prompt the ones are its first response slots, between 64 and 256 of them; in every draw some prompt has all 256 slots filled.
All inputs are finite; a program needn't handle non-finite values.
Results may differ from a plain program's by a relative error of at most 0.003.
Values may be sent and summed in bfloat16 or wider, within the bound.
A program may use at most 128 MiB of HBM per device.

v0:
```python
import jax
import jax.numpy as jnp
from jax import lax
from jax.sharding import PartitionSpec as P


def from_behind(value, axis, steps):
    count = lax.axis_size(axis)
    pairs = [(source, (source + steps) % count) for source in range(count)]
    return lax.ppermute(value, axis, pairs)


def shards(embeddings, head_weight, valid_mask):
    group_size = lax.axis_size("resp")
    own_index = lax.axis_index("resp")
    prompts, block_rows, features = embeddings.shape
    halfway = group_size // 2
    valid_rows = valid_mask.astype(jnp.float32)
    counts = lax.psum(jnp.sum(valid_rows, axis=1), "resp")
    flat_rows = embeddings.reshape(prompts * block_rows, features)
    rows_in = lax.all_gather(head_weight, "resp", axis=0, tiled=True)
    direct = jnp.dot(flat_rows, rows_in, preferred_element_type=jnp.float32)
    partial_value = lax.dot_general(
        flat_rows, rows_in, (((1,), (1,)), ((), ())), preferred_element_type=jnp.float32
    )
    mirror = partial_value
    direct, mirror = (direct, mirror)
    projected = (direct - mirror).astype(jnp.bfloat16).reshape(prompts, block_rows, features)
    is_giver = own_index < halfway

    def pair_scores(block):
        return -jnp.einsum("prd,pqd->prq", embeddings, block, preferred_element_type=jnp.float32)

    def score_pair(block):
        return pair_scores(block)

    def record(scores_acc, outbox, block, distance):
        column = jnp.mod(own_index + distance, group_size)
        pair_tile = score_pair(block)
        at_middle = distance == halfway
        keep_it = jnp.logical_or(jnp.logical_not(at_middle), is_giver)
        kept_tile = jnp.where(keep_it, pair_tile, 0.0)
        scores_acc = lax.dynamic_update_slice_in_dim(
            scores_acc, kept_tile[:, :, None, :], column, 2
        )
        send_near = jnp.logical_and(distance > 0, distance < halfway)
        send_it = jnp.logical_or(send_near, jnp.logical_and(at_middle, is_giver))
        mirrored_tile = jnp.where(send_it, -jnp.swapaxes(pair_tile, 1, 2), 0.0)
        outbox = lax.dynamic_update_slice_in_dim(outbox, mirrored_tile[None], column, 0)
        return (scores_acc, outbox)

    scores_acc = jnp.zeros((prompts, block_rows, group_size, block_rows), jnp.float32)
    outbox = jnp.zeros((group_size, prompts, block_rows, block_rows), jnp.float32)
    scores_acc, outbox = record(scores_acc, outbox, projected, jnp.int32(0))

    def advance(turn, loop_state):
        moving, scores_now, outbox_now = loop_state
        moving = from_behind(moving, "resp", -1)
        scores_now, outbox_now = record(scores_now, outbox_now, moving, turn)
        return (moving, scores_now, outbox_now)

    final_state = lax.fori_loop(1, halfway + 1, advance, (projected, scores_acc, outbox))
    scores_acc, outbox = (final_state[1], final_state[2])
    returned = lax.all_to_all(
        outbox.astype(jnp.bfloat16), "resp", split_axis=0, concat_axis=0, tiled=True
    ).astype(outbox.dtype)
    combined = scores_acc + jnp.transpose(returned, (1, 2, 0, 3))
    combined = combined.reshape(prompts, block_rows, group_size * block_rows)
    column_ids = jnp.arange(group_size * block_rows, dtype=jnp.float32)
    valid_cols = (column_ids[None, :] < counts[:, None]).astype(jnp.float32)
    preferences = jax.nn.sigmoid(combined) * valid_rows[:, :, None] * valid_cols[:, None, :]
    totals = jnp.sum(preferences, axis=2) - 0.5 * valid_rows
    win_rates = valid_rows * totals / jnp.maximum(counts - 1.0, 1.0)[:, None]
    return (preferences, win_rates)


def solution(mesh):
    return jax.shard_map(
        shards,
        mesh=mesh,
        in_specs=(P("prompt", "resp", None), P("resp", None), P("prompt", "resp")),
        out_specs=(P("prompt", "resp", None), P("prompt", "resp")),
        check_vma=False,
    )
```

profile of v0, /device:TPU:0, one launch (start us, length us, event | category | flops | bytes accessed | tf_op | source)
XLA Modules:
  0.0 398.6 jit_solution(5785818249483482035)
XLA Ops:
  7.2 0.0 copy-start
  7.2 0.0 copy-start.1
  7.2 0.0 all-gather.2.cloned.1.call-start
  7.2 0.7 all-gather.2.cloned.1.call-update
  7.9 0.0 copy-done
  7.9 0.1 convert_reduce_fusion
  8.0 18.2 %psum.7 = f32[8]{0:T(128)S(1)} all-reduce(f32[8]{0:T(128)S(1)} %convert_reduce_fusion), channel_id=1, replica_groups=mesh['prompt'=4,'resp'=8] {'resp'}, use_global_device_ids=true, to_apply=%region_3.4 | all-reduce | flops 8 | bytes 64 | tf_op jit(solution)/shard_map/psum | solution.py:19
  26.2 0.1 broadcast_in_dim.53
  26.4 0.1 fusion.6
  26.4 210.1 %all-gather.2.cloned.1.call-done = bf16[3584,3584]{1,0:T(8,128)(2,1)} async-done(((bf16[448,3584]{1,0:T(8,128)(2,1)}), bf16[3584,3584]{1,0:T(8,128)(2,1)}) %all-gather.2.cloned.1.call-update) | async-done | bytes 25690128 | tf_op jit(solution)/shard_map/all_gather | solution.py:21
  236.5 0.0 copy-done.1
  236.5 13.6 %fusion.8 = f32[256,3584]{1,0:T(8,128)} fusion(bf16[256,3584]{1,0:T(8,128)(2,1)S(1)} %bitcast.45, bf16[3584,3584]{1,0:T(8,128)(2,1)} %all-gather.2.cloned.1.call-done), kind=kOutput, calls=%fused_computation.22 | convolution fusion | flops 6576668672 | bytes 31195136 | tf_op jit(solution)/shard_map/dot_general | solution.py:22
  250.1 14.6 %fusion = bf16[256,3584]{1,0:T(8,128)(2,1)} fusion(f32[256,3584]{1,0:T(8,128)} %fusion.8, bf16[256,3584]{1,0:T(8,128)(2,1)S(1)} %bitcast.46, bf16[3584,3584]{1,0:T(8,128)(2,1)} %all-gather.2.cloned.1.call-done), kind=kOutput, calls=%fused_computation.3 | convolution fusion | flops 6578503680 | bytes 33030144 | tf_op jit(solution)/shard_map/dot_general | solution.py:23
  264.7 2.1 fusion.1
  266.8 0.1 copy.5
  266.9 0.1 broadcast_in_dim.51
  267.1 109.0 %while.19 = (s32[]{:T(128)}, bf16[8,32,3584]{2,1,0:T(8,128)(2,1)}, f32[8,32,8,32]{3,1,0,2:T(8,128)S(1)}, bf16[8,8,32,32]{2,3,1,0:T(8,128)(2,1)S(1)}, pred[]{:T(5...) while((s32[]{:T(128)}, bf16[8,32,3584]{2,1,0:T(8,128)(2,1)}, ...), condition=%wide.region_1.0_spmd, body=%wide.region_0.0_spmd.sunk | while | flops 58753044 | bytes 15008107 | solution.py:62
  267.1 0.2 collective-permute-start
  267.3 21.1 %collective-permute-done = bf16[8,32,3584]{2,1,0:T(8,128)(2,1)S(1)} collective-permute-done((bf16[8,32,3584]{2,1,0:T(8,128)(2,1)}, bf16[8,32,3584]{2,1,0:T(8,128)(2,1)S(1)}, u32[]{:S(2)}, u32[]{:S(2)}) %collective-permute-start) | collective-permute-done | bytes 1835040 | tf_op jit(solution)/shard_map/while/body/eval_jaxpr/ppermute | solution.py:10
  288.4 2.1 bitcast_dynamic-update-slice_fusion.4
  290.5 1.3 copy.21
  291.8 3.6 collective-permute-start
  295.4 21.1 %collective-permute-done = bf16[8,32,3584]{2,1,0:T(8,128)(2,1)S(1)} collective-permute-done((bf16[8,32,3584]{2,1,0:T(8,128)(2,1)}, bf16[8,32,3584]{2,1,0:T(8,128)(2,1)S(1)}, u32[]{:S(2)}, u32[]{:S(2)}) %collective-permute-start) | collective-permute-done | bytes 1835040 | tf_op jit(solution)/shard_map/while/body/eval_jaxpr/ppermute | solution.py:10
  316.5 2.1 bitcast_dynamic-update-slice_fusion.4
  318.6 1.3 copy.21
  319.9 3.6 collective-permute-start
  323.5 21.1 %collective-permute-done = bf16[8,32,3584]{2,1,0:T(8,128)(2,1)S(1)} collective-permute-done((bf16[8,32,3584]{2,1,0:T(8,128)(2,1)}, bf16[8,32,3584]{2,1,0:T(8,128)(2,1)S(1)}, u32[]{:S(2)}, u32[]{:S(2)}) %collective-permute-start) | collective-permute-done | bytes 1835040 | tf_op jit(solution)/shard_map/while/body/eval_jaxpr/ppermute | solution.py:10
  344.6 2.1 bitcast_dynamic-update-slice_fusion.4
  346.7 1.3 copy.21
  348.0 3.6 collective-permute-start
  351.6 21.1 %collective-permute-done = bf16[8,32,3584]{2,1,0:T(8,128)(2,1)S(1)} collective-permute-done((bf16[8,32,3584]{2,1,0:T(8,128)(2,1)}, bf16[8,32,3584]{2,1,0:T(8,128)(2,1)S(1)}, u32[]{:S(2)}, u32[]{:S(2)}) %collective-permute-start) | collective-permute-done | bytes 1835040 | tf_op jit(solution)/shard_map/while/body/eval_jaxpr/ppermute | solution.py:10
  372.7 2.1 bitcast_dynamic-update-slice_fusion.4
  374.8 1.3 copy.21
  376.1 1.2 reshape.45
  377.3 4.9 %all-to-all-start = ((bf16[8,2,4096]{2,1,0:T(2,128)(2,1)}), bf16[8,2,4096]{2,1,0:T(2,128)(2,1)S(1)}, u32[]{:S(2)}, u32[]{:S(2)}) async-start(bf16[8,2,4096]{2,1,0:T(2,128)(2,1)} %reshape.45), calls=%async_computation | async-start | bytes 262144 | tf_op jit(solution)/shard_map/all_to_all | solution.py:64
  382.2 0.1 compare_convert_fusion
  382.2 0.3 copy.6
  382.6 6.3 %all-to-all-done = bf16[8,2,4096]{2,1,0:T(2,128)(2,1)S(1)} async-done(((bf16[8,2,4096]{2,1,0:T(2,128)(2,1)}), bf16[8,2,4096]{2,1,0:T(2,128)(2,1)S(1)}, u32[]{:S(2)}, u32[]{:S(2)}) %all-to-all-start) | async-done | bytes 131104 | tf_op jit(solution)/shard_map/all_to_all | solution.py:64
  388.9 0.3 reshape.46
  389.2 0.4 multiply_reduce_fusion
  389.6 0.4 copy.7
  389.9 0.3 div.16
  390.3 0.8 multiply_multiply_fusion
  391.1 0.7 multiply_divide_fusion
  (9 shorter events, 0.2 us)
Async XLA Ops:
  7.2 0.8 copy-start
  7.2 229.4 %copy-start.1 = (bf16[8,32,3584]{2,1,0:T(8,128)(2,1)S(1)}, bf16[8,32,3584]{2,1,0:T(8,128)(2,1)}, u32[]{:S(2)}) copy-start(bf16[8,32,3584]{2,1,0:T(8,128)(2,1)} %param.5) | copy-start | bytes 5505028
  7.2 229.3 %all-gather.2.cloned.1.call-start = ((), (), s32[]{:S(2)}) async-start(), calls=%async_computation.1 | async-start | bytes 28901376 | tf_op jit(solution)/shard_map/all_gather | solution.py:21
  267.1 21.3 %collective-permute-start = (bf16[8,32,3584]{2,1,0:T(8,128)(2,1)}, bf16[8,32,3584]{2,1,0:T(8,128)(2,1)S(1)}, u32[]{:S(2)}, u32[]{:S(2)}) collective-permute-start(bf16[8,32,3584]{2,1,0:T(8,128)(2,1)} %get-tuple-element.262), channel_id=1, source_target_pairs={{0,7},{1,0},{2,1},{3,2},{4,3},{5,4},{6,5},{7,6},{8,15},{9,8},{10,9... | collective-permute-start | bytes 5505032 | tf_op jit(solution)/shard_map/while/body/eval_jaxpr/ppermute | solution.py:10
  291.8 24.7 %collective-permute-start = (bf16[8,32,3584]{2,1,0:T(8,128)(2,1)}, bf16[8,32,3584]{2,1,0:T(8,128)(2,1)S(1)}, u32[]{:S(2)}, u32[]{:S(2)}) collective-permute-start(bf16[8,32,3584]{2,1,0:T(8,128)(2,1)} %get-tuple-element.262), channel_id=1, source_target_pairs={{0,7},{1,0},{2,1},{3,2},{4,3},{5,4},{6,5},{7,6},{8,15},{9,8},{10,9... | collective-permute-start | bytes 5505032 | tf_op jit(solution)/shard_map/while/body/eval_jaxpr/ppermute | solution.py:10
  319.9 24.7 %collective-permute-start = (bf16[8,32,3584]{2,1,0:T(8,128)(2,1)}, bf16[8,32,3584]{2,1,0:T(8,128)(2,1)S(1)}, u32[]{:S(2)}, u32[]{:S(2)}) collective-permute-start(bf16[8,32,3584]{2,1,0:T(8,128)(2,1)} %get-tuple-element.262), channel_id=1, source_target_pairs={{0,7},{1,0},{2,1},{3,2},{4,3},{5,4},{6,5},{7,6},{8,15},{9,8},{10,9... | collective-permute-start | bytes 5505032 | tf_op jit(solution)/shard_map/while/body/eval_jaxpr/ppermute | solution.py:10
  348.0 24.7 %collective-permute-start = (bf16[8,32,3584]{2,1,0:T(8,128)(2,1)}, bf16[8,32,3584]{2,1,0:T(8,128)(2,1)S(1)}, u32[]{:S(2)}, u32[]{:S(2)}) collective-permute-start(bf16[8,32,3584]{2,1,0:T(8,128)(2,1)} %get-tuple-element.262), channel_id=1, source_target_pairs={{0,7},{1,0},{2,1},{3,2},{4,3},{5,4},{6,5},{7,6},{8,15},{9,8},{10,9... | collective-permute-start | bytes 5505032 | tf_op jit(solution)/shard_map/while/body/eval_jaxpr/ppermute | solution.py:10
  377.3 11.6 %all-to-all-start = ((bf16[8,2,4096]{2,1,0:T(2,128)(2,1)}), bf16[8,2,4096]{2,1,0:T(2,128)(2,1)S(1)}, u32[]{:S(2)}, u32[]{:S(2)}) async-start(bf16[8,2,4096]{2,1,0:T(2,128)(2,1)} %reshape.45), calls=%async_computation | async-start | bytes 262144 | tf_op jit(solution)/shard_map/all_to_all | solution.py:64
Sparse Core Ops, SparseCore 0:
  9.6 226.8 all-gather.1
where the time goes:
time: 399 us
  waiting for transfers between devices  301 us (75%)
  matrix products  38.8 us (10%)
  blocking collectives  18.2 us (5%)
  starting transfers between devices  15.9 us (4%)
  between operations  14.1 us (4%)
  local copies, waits for them, and re-layouts  7.94 us (2%)
    all_gather x1, waiting for transfers between devices, shards(): rows_in = lax.all_gather(head_weight, 'resp', axis=0, tiled=True)  210 us
    ppermute x4, waiting for transfers between devices, from_behind(): return lax.ppermute(value, axis, pairs)  84.2 us
    psum x1, blocking collectives, shards(): counts = lax.psum(jnp.sum(valid_rows, axis=1), 'resp')  18.2 us
    dot_general x1, matrix products, shards(): lax.dot_general(flat_rows, rows_in, (((1,), (1,)), ((), ())), preferred_e...  14.6 us
    dot_general x1, matrix products, shards(): direct = jnp.dot(flat_rows, rows_in, preferred_element_type=jnp.float32)  13.6 us
    ppermute x4, starting transfers between devices, from_behind(): return lax.ppermute(value, axis, pairs)  11 us
    dot_general x5, matrix products, pair_scores(): jnp.einsum('prd,pqd->prq', embeddings, block, preferred_element_type=jnp....  10.6 us
  transfers between devices with their start and end apart: 6, of which 6 were waited for; matrix products, arithmetic and copies ran while one was open for 0% of the time, Pallas kernels for 0%

commit v1 on v0

v1 whole, which is shorter than its diff:
```python
import jax
import jax.numpy as jnp
from jax import lax
from jax.sharding import PartitionSpec as P


def halves_of_scores(embeddings, head_weight, own_index, group_size):
    prompts, block_rows, features = embeddings.shape
    held = head_weight.shape[0]
    slots = group_size * block_rows
    everyone = lax.all_gather(embeddings, "resp", axis=0, tiled=True)
    flat = everyone.reshape(group_size * prompts * block_rows, features)
    through = lax.dot_general(
        flat, head_weight, (((1,), (1,)), ((), ())), preferred_element_type=jnp.float32
    ).astype(jnp.bfloat16)
    through = through.reshape(group_size, prompts, block_rows, held)
    mine = lax.dynamic_slice_in_dim(
        everyone.reshape(group_size, prompts, block_rows, features), own_index * held, held, 3
    )
    partial = jnp.einsum("gpid,hpjd->gpihj", mine, through, preferred_element_type=jnp.float32)
    flipped = jnp.einsum("gpid,hpjd->gpihj", through, mine, preferred_element_type=jnp.float32)
    partial = (partial - flipped).astype(jnp.bfloat16)
    return partial.reshape(group_size, prompts, block_rows, slots)


def shards(embeddings, head_weight, valid_mask):
    group_size = lax.axis_size("resp")
    own_index = lax.axis_index("resp")
    prompts, block_rows, features = embeddings.shape
    slots = group_size * block_rows
    valid_rows = valid_mask.astype(jnp.float32)
    counts = lax.psum(jnp.sum(valid_rows, axis=1), "resp")
    at_once = max(1, min(prompts, (1 << 11) // slots))

    def scores_of(some):
        partial = halves_of_scores(some, head_weight, own_index, group_size)
        swapped = lax.all_to_all(partial, "resp", split_axis=0, concat_axis=0, tiled=True)
        return jnp.sum(swapped.astype(jnp.float32), axis=0)

    if at_once == prompts:
        scores = scores_of(embeddings)
    else:
        scores = lax.map(scores_of, embeddings.reshape(prompts // at_once, at_once, block_rows, features))
        scores = scores.reshape(prompts, block_rows, slots)
    column_ids = jnp.arange(slots, dtype=jnp.float32)
    valid_cols = (column_ids[None, :] < counts[:, None]).astype(jnp.float32)
    preferences = jax.nn.sigmoid(scores) * valid_rows[:, :, None] * valid_cols[:, None, :]
    totals = jnp.sum(preferences, axis=2) - 0.5 * valid_rows
    win_rates = valid_rows * totals / jnp.maximum(counts - 1.0, 1.0)[:, None]
    return (preferences, win_rates)


def solution(mesh):
    return jax.shard_map(
        shards,
        mesh=mesh,
        in_specs=(P("prompt", "resp", None), P("resp", None), P("prompt", "resp")),
        out_specs=(P("prompt", "resp", None), P("prompt", "resp")),
        check_vma=False,
    )
```

time: 399 us -> 229 us (0.57)
  waiting for transfers between devices: 301 us -> 139 us
  matrix products: 38.8 us -> 21.8 us
  starting transfers between devices: 15.9 us -> 4.27 us
  blocking collectives: 18.2 us -> 29.2 us
  local copies, waits for them, and re-layouts: 7.94 us -> 16.8 us
    ppermute x4 -> x0, waiting for transfers between devices: 84.2 us -> none  [from_behind(): return lax.ppermute(value, axis, pairs)]
    all_gather x1, waiting for transfers between devices: 210 us -> 138 us  [halves_of_scores(): everyone = lax.all_gather(embeddings, 'resp', axis=0, tiled=True)]
    dot_general x7 -> x3, matrix products: 38.8 us -> 21.8 us  [the longest x1 11.1 us: halves_of_scores(): lax.dot_general(flat, head_weight, (((1,), (1,)), ((), ())), preferred_el...]
    ppermute x4 -> x0, starting transfers between devices: 11 us -> none  [from_behind(): return lax.ppermute(value, axis, pairs)]
    psum x1, blocking collectives: 18.2 us -> 29.2 us  [shards(): counts = lax.psum(jnp.sum(valid_rows, axis=1), 'resp')]
    convert_element_type x0 -> x2, local copies, waits for them, and re-layouts: none -> 10.6 us  [the longest x1 6.77 us: halves_of_scores(): partial = (partial - flipped).astype(jnp.bfloat16)]
    all_to_all x1, waiting for transfers between devices: 6.32 us -> 0.01 us  [scores_of(): lax.all_to_all(partial, 'resp', split_axis=0, concat_axis=0, tiled=True)]
    reshape x0 -> x1, local copies, waits for them, and re-layouts: none -> 6.19 us  [halves_of_scores(): return partial.reshape(group_size, prompts, block_rows, slots)]
  transfers between devices with their start and end apart: 6 -> 2, of which waited for: 6 -> 1; matrix products, arithmetic and copies ran while one was open for 0% -> 0% of each run, Pallas kernels for 0% -> 0%
where the time goes in v1:
time: 229 us; the launch traced here: 228 us
  waiting for transfers between devices  139 us (61%)
  blocking collectives  29.2 us (13%)
  matrix products  21.8 us (10%)
  local copies, waits for them, and re-layouts  16.8 us (7%)
  between operations  14.1 us (6%)
  starting transfers between devices  4.27 us (2%)
  other arithmetic  3.09 us (1%)
    all_gather x1, waiting for transfers between devices, halves_of_scores(): everyone = lax.all_gather(embeddings, 'resp', axis=0, tiled=True)  138 us
    psum x1, blocking collectives, shards(): counts = lax.psum(jnp.sum(valid_rows, axis=1), 'resp')  29.2 us
    dot_general x1, matrix products, halves_of_scores(): lax.dot_general(flat, head_weight, (((1,), (1,)), ((), ())), preferred_el...  11.1 us
    convert_element_type x1, local copies, waits for them, and re-layouts, halves_of_scores(): partial = (partial - flipped).astype(jnp.bfloat16)  6.77 us
    reshape x1, local copies, waits for them, and re-layouts, halves_of_scores(): return partial.reshape(group_size, prompts, block_rows, slots)  6.19 us
    dot_general x1, matrix products, halves_of_scores(): jnp.einsum('gpid,hpjd->gpihj', through, mine, preferred_element_type=jnp....  5.82 us
    dot_general x1, matrix products, halves_of_scores(): jnp.einsum('gpid,hpjd->gpihj', mine, through, preferred_element_type=jnp....  4.94 us
  transfers between devices with their start and end apart: 2, of which 1 were waited for; matrix products, arithmetic and copies ran while one was open for 0% of the time, Pallas kernels for 0%

profile of v1, /device:TPU:0, one launch (start us, length us, event | category | flops | bytes accessed | tf_op | source)
XLA Modules:
  0.0 228.3 jit_solution(2787483012243763195)
XLA Ops:
  7.2 0.0 copy-start
  7.2 0.0 all-gather.2.cloned.1.call-start
  7.2 0.7 all-gather.2.cloned.1.call-update
  7.9 138.4 %all-gather.2.cloned.1.call-done = bf16[64,32,3584]{2,1,0:T(8,128)(2,1)} async-done(((bf16[8,32,3584]{2,1,0:T(8,128)(2,1)}), bf16[64,32,3584]{2,1,0:T(8,128)(2,1)}) %all-gather.2.cloned.1.call-update) | async-done | bytes 14680080 | tf_op jit(solution)/shard_map/all_gather | solution.py:11
  146.3 0.0 copy-done
  146.3 11.1 %convolution_convert_fusion = bf16[2048,448]{0,1:T(8,128)(2,1)} fusion(bf16[2048,3584]{1,0:T(8,128)(2,1)} %bitcast.23, bf16[448,3584]{1,0:T(8,128)(2,1)S(1)} %copy-done), kind=kOutput, calls=%fused_computation.2 | convolution fusion | flops 6577586176 | bytes 19726336 | tf_op jit(solution)/shard_map/dot_general | solution.py:13
  157.3 3.8 %copy.12 = bf16[2048,448]{1,0:T(8,128)(2,1)} copy(bf16[2048,448]{0,1:T(8,128)(2,1)} %convolution_convert_fusion) | data formatting | bytes 3670016 | tf_op jit(solution)/shard_map/convert_element_type | solution.py:15
  161.2 0.0 copy-start.1
  161.2 4.9 %fusion.2 = f32[8,8,32,8,32]{4,2,3,1,0:T(8,128)S(1)} fusion(bf16[8,8,32,448,1]{3,2,1,0,4:T(8,128)(2,1)} %bitcast.21, bf16[8,8,32,3584]{3,2,1,0:T(8,128)(2,1)} %bitcast.24, s32[]{:T(128)S(6)} %select_n.3), kind=kOutput, calls=%fused_computation.4 | convolution fusion | flops 469762048 | bytes 6291460 | tf_op jit(solution)/shard_map/gpid,hpjd->gpihj/dot_general | solution.py:20
  166.1 0.0 copy-done.1
  166.1 5.8 %fusion = bf16[8,8,32,8,32]{2,4,0,3,1:T(8,128)(2,1)} fusion(f32[8,8,32,8,32]{4,2,3,1,0:T(8,128)S(1)} %fusion.2, bf16[8,8,32,448,1]{3,2,1,0,4:T(8,128)(2,1)S(1)} %bitcast.22, bf16[8,8,32,3584]{3,2,1,0:T(8,128)(2,1)} %bitcast.25, s32[]{:T(128)S(6)} %select_n.3), kind=kOutput, calls=%fused_computation.1 | convolution fusion | flops 470810624 | bytes 7077892 | tf_op jit(solution)/shard_map/gpid,hpjd->gpihj/dot_general | solution.py:21
  171.9 6.8 %copy.16 = bf16[8,8,32,8,32]{4,3,2,1,0:T(8,128)(2,1)} copy(bf16[8,8,32,8,32]{2,4,0,3,1:T(8,128)(2,1)} %fusion) | data formatting | bytes 2097152 | tf_op jit(solution)/shard_map/convert_element_type | solution.py:22
  178.7 0.0 copy-start.2
  178.7 6.2 %reshape.39 = bf16[8,8,32,256]{3,2,1,0:T(8,128)(2,1)} reshape(bf16[8,8,32,8,32]{4,3,2,1,0:T(8,128)(2,1)} %copy.16) | data formatting | bytes 2097152 | tf_op jit(solution)/shard_map/reshape | solution.py:23
  184.9 4.2 %all-to-all-start = ((bf16[8,8,32,256]{3,2,1,0:T(8,128)(2,1)}), bf16[8,8,32,256]{3,2,1,0:T(8,128)(2,1)}, u32[]{:S(2)}, u32[]{:S(2)}) async-start(bf16[8,8,32,256]{3,2,1,0:T(8,128)(2,1)} %reshape.39), calls=%async_computation | async-start | bytes 2097152 | tf_op jit(solution)/shard_map/all_to_all | solution.py:37
  189.1 0.0 copy-done.2
  189.1 0.1 convert_reduce_fusion.1
  189.3 29.2 %psum.7 = f32[8]{0:T(128)S(1)} all-reduce(f32[8]{0:T(128)S(1)} %convert_reduce_fusion.1), channel_id=1, replica_groups=mesh['prompt'=4,'resp'=8] {'resp'}, use_global_device_ids=true, to_apply=%region_2.0 | all-reduce | flops 8 | bytes 64 | tf_op jit(solution)/shard_map/psum | solution.py:32
  218.5 0.1 fusion.8
  218.5 0.0 all-to-all-done
  218.5 1.4 convert_reduce_fusion
  220.0 0.8 fusion.9
  220.8 0.7 multiply_divide_fusion
  (2 shorter events, 0.0 us)
Async XLA Ops:
  7.2 139.1 %copy-start = (bf16[448,3584]{1,0:T(8,128)(2,1)S(1)}, bf16[448,3584]{1,0:T(8,128)(2,1)}, u32[]{:S(2)}) copy-start(bf16[448,3584]{1,0:T(8,128)(2,1)} %param.4) | copy-start | bytes 9633796
  7.2 139.1 %all-gather.2.cloned.1.call-start = ((), (), s32[]{:S(2)}) async-start(), calls=%async_computation.1 | async-start | bytes 16515072 | tf_op jit(solution)/shard_map/all_gather | solution.py:11
  161.2 4.9 %copy-start.1 = (bf16[2048,448]{1,0:T(8,128)(2,1)S(1)}, bf16[2048,448]{1,0:T(8,128)(2,1)}, u32[]{:S(2)}) copy-start(bf16[2048,448]{1,0:T(8,128)(2,1)} %copy.12) | copy-start | bytes 5505028
  178.7 10.4 %copy-start.2 = (s32[8,32]{1,0:T(8,128)S(1)}, s32[8,32]{1,0:T(8,128)}, u32[]{:S(2)}) copy-start(s32[8,32]{1,0:T(8,128)} %param.5) | copy-start | bytes 3076
  184.9 33.6 %all-to-all-start = ((bf16[8,8,32,256]{3,2,1,0:T(8,128)(2,1)}), bf16[8,8,32,256]{3,2,1,0:T(8,128)(2,1)}, u32[]{:S(2)}, u32[]{:S(2)}) async-start(bf16[8,8,32,256]{3,2,1,0:T(8,128)(2,1)} %reshape.39), calls=%async_computation | async-start | bytes 2097152 | tf_op jit(solution)/shard_map/all_to_all | solution.py:37
Sparse Core Ops, SparseCore 0:
  9.6 136.6 all-gather.1

commit v2 on v1

v2 whole, which is shorter than its diff:
```python
import functools

import jax
import jax.numpy as jnp
from jax import lax
from jax.experimental import pallas as pl
from jax.experimental.pallas import tpu as pltpu
from jax.sharding import PartitionSpec as P

MESH = pl.DeviceIdType.MESH
CORES = 2
CHIPS = 4
PARTS = 4
NT = (((1,), (1,)), ((), ()))


def gathered_halves(embeddings, head_weight, own_index, group_size):
    prompts, block_rows, features = embeddings.shape
    held = head_weight.shape[0]
    slots = group_size * block_rows
    everyone = lax.all_gather(embeddings, "resp", axis=0, tiled=True)
    flat = everyone.reshape(group_size * prompts * block_rows, features)
    through = lax.dot_general(flat, head_weight, NT, preferred_element_type=jnp.float32)
    through = through.astype(jnp.bfloat16).reshape(group_size, prompts, block_rows, held)
    mine = lax.dynamic_slice_in_dim(
        everyone.reshape(group_size, prompts, block_rows, features), own_index * held, held, 3
    )
    partial = jnp.einsum("gpid,hpjd->gpihj", mine, through, preferred_element_type=jnp.float32)
    flipped = jnp.einsum("gpid,hpjd->gpihj", through, mine, preferred_element_type=jnp.float32)
    partial = (partial - flipped).astype(jnp.bfloat16)
    return partial.reshape(group_size, prompts, block_rows, slots)


def gathered_scores(embeddings, head_weight):
    group_size = lax.axis_size("resp")
    own_index = lax.axis_index("resp")
    prompts, block_rows, features = embeddings.shape
    slots = group_size * block_rows
    at_once = max(1, min(prompts, (1 << 11) // slots))

    def scores_of(some):
        partial = gathered_halves(some, head_weight, own_index, group_size)
        swapped = lax.all_to_all(partial, "resp", split_axis=0, concat_axis=0, tiled=True)
        return jnp.sum(swapped.astype(jnp.float32), axis=0)

    pieces = embeddings.reshape(prompts // at_once, at_once, block_rows, features)
    return lax.map(scores_of, pieces).reshape(prompts, block_rows, slots)


def kernel(e_ref, w_ref, m_ref, s_ref, g_ref,
           ebuf, wbuf, zbuf, sbuf, keep, pbuf, qbuf, fbuf, rbuf, mbuf,
           m_send, m_recv, e_send, e_recv, ef_send, el_sem,
           w_send, w_recv, wl_sem, p_send, p_recv, f_send, r_recv):
    part = lax.axis_index("prompt")
    me = lax.axis_index("resp")
    z = me // CORES
    core = me % CORES
    half = z // 2
    prompts, block_rows, features = e_ref.shape
    held = w_ref.shape[0]
    per_core = prompts // CORES
    group = CHIPS * CORES
    span = held * group // 2
    rows = group * block_rows
    half_rows = rows // 2
    z_in = 1 + half
    z_out = 3 * half
    z_far = 2 - half
    far_out = 3 - z_out
    inner = z == z_in
    quarter = held // PARTS
    width = 256 if span % 256 == 0 else span

    def copy(src, dst, send, recv, chip, c, q=None):
        return pltpu.make_async_remote_copy(
            src, dst, send, recv,
            device_id=(part if q is None else q, chip * CORES + c), device_id_type=MESH,
        )

    def arrived(dst, recv):
        copy(dst, dst, m_send.at[0], recv, z_far, core).wait_recv()

    others = [lax.rem(me + d, group) for d in range(1, group)]
    plane = [lax.rem(part + d, PARTS) for d in range(1, PARTS)]
    barrier = pltpu.get_barrier_semaphore()
    for other in others:
        pl.semaphore_signal(barrier, inc=1, device_id=(part, other), device_id_type=MESH)
    for q in plane:
        pl.semaphore_signal(barrier, inc=1, device_id=(q, me), device_id_type=MESH)
    pl.semaphore_wait(barrier, len(others) + len(plane))

    def w_rows(block, start, size):
        return wbuf.at[pl.ds(pl.multiple_of(block * held + start, 16), size)]

    def mask_copy(d):
        return pltpu.make_async_remote_copy(
            m_ref, mbuf.at[me], m_send.at[d], m_recv.at[me],
            device_id=(part, others[d]), device_id_type=MESH,
        )

    my_block = me - half * group // 2
    out_block = z_out * CORES + core - half * group // 2
    out_other = z_out * CORES + 1 - core - half * group // 2
    in_other = z_in * CORES + 1 - core - half * group // 2
    my_quarter = pl.multiple_of(part * quarter, 16)

    def outer_w():
        return copy(w_ref.at[pl.ds(my_quarter, quarter)], w_rows(my_block, my_quarter, quarter),
                    w_send.at[0], w_recv.at[part], z_in, core)

    def outer_e(j, c):
        return copy(e_ref.at[c * per_core + j], ebuf.at[j, me],
                    e_send.at[j, c], e_recv.at[j, me], z_in, c)

    def far_e(j, c):
        return copy(e_ref.at[c * per_core + j], ebuf.at[j, me],
                    e_send.at[j, c], e_recv.at[j, me], z_far, c)

    def near_e(j):
        return copy(e_ref.at[(1 - core) * per_core + j], ebuf.at[j, me],
                    e_send.at[j, 2], e_recv.at[j, me], z_in, 1 - core)

    def own_e(j):
        return pltpu.make_async_copy(e_ref.at[core * per_core + j], ebuf.at[j, me], el_sem.at[j])

    def onward_e(j, c):
        spot = ebuf.at[j, z_out * CORES + c]
        return copy(spot, spot, ef_send.at[j, c], e_recv.at[j, z_out * CORES + c], z_far, core)

    def near_w():
        return copy(w_ref, w_rows(my_block, 0, held), w_send.at[0], w_recv.at[PARTS], z_in, 1 - core)

    def own_w():
        return pltpu.make_async_copy(w_ref, w_rows(my_block, 0, held), wl_sem.at[0])

    def plane_w(d):
        spot = w_rows(out_block, my_quarter, quarter)
        return copy(spot, spot, w_send.at[1 + d], w_recv.at[part], z_in, core, plane[d])

    def across_w():
        spot = w_rows(out_block, 0, held)
        return copy(spot, spot, w_send.at[PARTS], w_recv.at[PARTS + 1], z_in, 1 - core)

    def partial_copy(j):
        return copy(pbuf.at[j], qbuf.at[j], p_send.at[j], p_recv.at[j], z_far, core)

    def final_copy(j, t):
        target = half * (group // 2) + lax.rem(my_block + 1 + t, group // 2)
        row = pl.multiple_of(lax.rem(my_block + 1 + t, group // 2) * block_rows, block_rows)
        return pltpu.make_async_remote_copy(
            fbuf.at[j, pl.ds(row, block_rows)], rbuf.at[core * per_core + j],
            f_send.at[j, t], r_recv.at[core * per_core + j],
            device_id=(part, target), device_id_type=MESH,
        )

    @pl.when(jnp.logical_not(inner))
    def _():
        outer_w().start()
        for j in range(per_core):
            for c in range(CORES):
                outer_e(j, c).start()

    @pl.when(inner)
    def _():
        for j in range(per_core):
            for c in range(CORES):
                far_e(j, c).start()
        near_w().start()
        for j in range(per_core):
            near_e(j).start()
        own_w().start()
        for j in range(per_core):
            own_e(j).start()

    for d in range(group - 1):
        mask_copy(d).start()
    mbuf[me] = m_ref[...]

    @pl.when(inner)
    def _():
        arrived(w_rows(out_block, my_quarter, quarter), w_recv.at[part])
        for d in range(PARTS - 1):
            plane_w(d).start()

        def pass_on(j, carry):
            for c in range(CORES):
                arrived(ebuf.at[j, z_out * CORES + c], e_recv.at[j, z_out * CORES + c])
                onward_e(j, c).start()
            return carry

        lax.fori_loop(0, per_core, pass_on, 0)
        for q in plane:
            arrived(w_rows(out_block, q * quarter, quarter), w_recv.at[q])
        across_w().start()
        own_w().wait()
        arrived(w_rows(in_other, 0, held), w_recv.at[PARTS])
        arrived(w_rows(out_other, 0, held), w_recv.at[PARTS + 1])

        mine_at = pl.multiple_of(half * half_rows, half_rows)
        theirs_at = pl.multiple_of((1 - half) * half_rows, half_rows)
        lanes = pl.ds(pl.multiple_of(half * span, 128), span)

        def finish(j):
            arrived(qbuf.at[j], p_recv.at[j])
            fbuf[j] = (keep[j] + qbuf[j].astype(jnp.float32)).astype(jnp.bfloat16)
            for t in range(group // 2 - 1):
                final_copy(j, t).start()
            own_row = pl.multiple_of(my_block * block_rows, block_rows)
            rbuf[core * per_core + j] = fbuf[j, pl.ds(own_row, block_rows)]

        def score(j, carry):
            own_e(j).wait()
            arrived(ebuf.at[j, z_in * CORES + 1 - core], e_recv.at[j, z_in * CORES + 1 - core])
            for chip in (z_far, far_out):
                for c in range(CORES):
                    arrived(ebuf.at[j, chip * CORES + c], e_recv.at[j, chip * CORES + c])

            def project(k, inside):
                start = pl.multiple_of(k * width, width)
                left = ebuf[j].reshape(rows, features)
                zbuf[:, pl.ds(start, width)] = lax.dot_general(
                    left, wbuf[pl.ds(start, width)], NT, preferred_element_type=jnp.float32
                ).astype(jnp.bfloat16)
                return inside

            lax.fori_loop(0, span // width, project, 0)
            left = ebuf[j, :, :, lanes].reshape(rows, span)
            right = zbuf[...]
            sbuf[...] = lax.dot_general(
                left, right, NT, preferred_element_type=jnp.float32
            ) - lax.dot_general(right, left, NT, preferred_element_type=jnp.float32)
            pbuf[j] = sbuf[pl.ds(theirs_at, half_rows)].astype(jnp.bfloat16)
            partial_copy(j).start()
            keep[j] = sbuf[pl.ds(mine_at, half_rows)]

            @pl.when(j > 0)
            def _():
                finish(j - 1)

            return carry

        lax.fori_loop(0, per_core, score, 0)
        finish(per_core - 1)
        for j in range(per_core):
            arrived(rbuf.at[(1 - core) * per_core + j], r_recv.at[(1 - core) * per_core + j])
        for j in range(per_core):
            for c in range(CORES):
                far_e(j, c).wait_send()
                onward_e(j, c).wait_send()
            near_e(j).wait_send()
            partial_copy(j).wait_send()
            for t in range(group // 2 - 1):
                final_copy(j, t).wait_send()
        near_w().wait_send()
        across_w().wait_send()
        for d in range(PARTS - 1):
            plane_w(d).wait_send()

    @pl.when(jnp.logical_not(inner))
    def _():
        outer_w().wait_send()
        for j in range(per_core):
            for c in range(CORES):
                outer_e(j, c).wait_send()
        for p in range(prompts):
            arrived(rbuf.at[p], r_recv.at[p])

    for d in range(group - 1):
        mask_copy(d).wait_send()
        arrived(mbuf.at[others[d]], m_recv.at[others[d]])
    s_ref[...] = rbuf[...]
    g_ref[...] = mbuf[...]


def line_scores(embeddings, head_weight, mask):
    prompts, block_rows, features = embeddings.shape
    held = head_weight.shape[0]
    group = CHIPS * CORES
    per_core = prompts // CORES
    span = held * group // 2
    rows = group * block_rows
    half_rows = rows // 2
    bf16, f32 = jnp.bfloat16, jnp.float32
    dma = pltpu.SemaphoreType.DMA
    anywhere = pl.BlockSpec(memory_space=pl.ANY)
    vmem = pl.BlockSpec(memory_space=pltpu.VMEM)
    padded = jnp.pad(mask, ((0, 0), (0, 128 - block_rows)))
    return pl.pallas_call(
        kernel,
        out_shape=(
            jax.ShapeDtypeStruct((prompts, block_rows, rows), bf16),
            jax.ShapeDtypeStruct((group, prompts, 128), jnp.int32),
        ),
        in_specs=[anywhere, anywhere, vmem],
        out_specs=(vmem, vmem),
        scratch_shapes=[
            pltpu.VMEM((per_core, group, block_rows, features), bf16),
            pltpu.VMEM((span, features), bf16),
            pltpu.VMEM((rows, span), bf16),
            pltpu.VMEM((rows, rows), f32),
            pltpu.VMEM((per_core, half_rows, rows), f32),
            pltpu.VMEM((per_core, half_rows, rows), bf16),
            pltpu.VMEM((per_core, half_rows, rows), bf16),
            pltpu.VMEM((per_core, half_rows, rows), bf16),
            pltpu.VMEM((prompts, block_rows, rows), bf16),
            pltpu.VMEM((group, prompts, 128), jnp.int32),
            dma((group - 1,)),
            dma((group,)),
            dma((per_core, 3)),
            dma((per_core, group)),
            dma((per_core, CORES)),
            dma((per_core,)),
            dma((PARTS + 1,)),
            dma((PARTS + 2,)),
            dma((1,)),
            dma((per_core,)),
            dma((per_core,)),
            dma((per_core, group // 2 - 1)),
            dma((prompts,)),
        ],
        compiler_params=pltpu.CompilerParams(
            collective_id=0, has_side_effects=True, vmem_limit_bytes=56 << 20
        ),
    )(embeddings, head_weight, padded)


def shards(embeddings, head_weight, valid_mask):
    group_size = lax.axis_size("resp")
    prompts, block_rows, features = embeddings.shape
    slots = group_size * block_rows
    valid_rows = valid_mask.astype(jnp.float32)
    if (lax.axis_size("prompt"), group_size) == (PARTS, CHIPS * CORES):
        scores, masks = line_scores(embeddings, head_weight, valid_mask)
        scores = scores.astype(jnp.float32)
        valid_cols = jnp.transpose(masks[:, :, :block_rows], (1, 0, 2)).reshape(prompts, slots)
        valid_cols = valid_cols.astype(jnp.float32)
        counts = jnp.sum(valid_cols, axis=1)
    else:
        counts = lax.psum(jnp.sum(valid_rows, axis=1), "resp")
        scores = gathered_scores(embeddings, head_weight)
        column_ids = jnp.arange(slots, dtype=jnp.float32)
        valid_cols = (column_ids[None, :] < counts[:, None]).astype(jnp.float32)
    preferences = jax.nn.sigmoid(scores) * valid_rows[:, :, None] * valid_cols[:, None, :]
    totals = jnp.sum(preferences, axis=2) - 0.5 * valid_rows
    win_rates = valid_rows * totals / jnp.maximum(counts - 1.0, 1.0)[:, None]
    return (preferences, win_rates)


def solution(mesh):
    return jax.shard_map(
        shards,
        mesh=mesh,
        in_specs=(P("prompt", "resp", None), P("resp", None), P("prompt", "resp")),
        out_specs=(P("prompt", "resp", None), P("prompt", "resp")),
        check_vma=False,
    )
```

time: 229 us -> 115 us (0.50)
  waiting for transfers between devices: 139 us -> 0 us
  Pallas kernels: 0 us -> 107 us
  blocking collectives: 29.2 us -> 0 us
  matrix products: 21.8 us -> 0 us
  local copies, waits for them, and re-layouts: 16.8 us -> 1.38 us
  between operations: 14.1 us -> 0.65 us
  starting transfers between devices: 4.27 us -> 0 us
    all_gather x1 -> x0, waiting for transfers between devices: 138 us -> none  [halves_of_scores(): everyone = lax.all_gather(embeddings, 'resp', axis=0, tiled=True)]
    pallas_call x0 -> x1, Pallas kernels: none -> 107 us  [line_scores(): pl.pallas_call(kernel, out_shape=(jax.ShapeDtypeStruct((prompts, block_ro...]
    psum x1 -> x0, blocking collectives: 29.2 us -> none  [shards(): counts = lax.psum(jnp.sum(valid_rows, axis=1), 'resp')]
    dot_general x3 -> x0, matrix products: 21.8 us -> none  [the longest x1 11.1 us: halves_of_scores(): lax.dot_general(flat, head_weight, (((1,), (1,)), ((), ())), preferred_el...]
    convert_element_type x2, local copies, waits for them, and re-layouts: 10.6 us -> 0.09 us  [shards(): valid_cols = valid_cols.astype(jnp.float32)]
    reshape x1 -> x0, local copies, waits for them, and re-layouts: 6.19 us -> none  [halves_of_scores(): return partial.reshape(group_size, prompts, block_rows, slots)]
    all_to_all x1 -> x0, starting transfers between devices: 4.23 us -> none  [scores_of(): lax.all_to_all(partial, 'resp', split_axis=0, concat_axis=0, tiled=True)]
  transfers between devices with their start and end apart: 2 -> 0, of which waited for: 1 -> 0; matrix products, arithmetic and copies ran while one was open for 0% -> 0% of each run, Pallas kernels for 0% -> 0%
where the time goes in v2:
time: 115 us; the launch traced here: 114 us
  Pallas kernels  107 us (93%)
  other arithmetic  4.78 us (4%)
  local copies, waits for them, and re-layouts  1.38 us (1%)
    pallas_call x1, Pallas kernels, line_scores(): pl.pallas_call(kernel, out_shape=(jax.ShapeDtypeStruct((prompts, block_ro...  107 us

profile of v2, /device:TPU:0, one launch (start us, length us, event | category | flops | bytes accessed | tf_op | source)
XLA Modules:
  0.0 114.2 jit_solution(15097043821985381421)
XLA Ops:
  0.6 0.0 copy-start
  0.6 0.8 convert_element_type.22
  1.4 1.3 %pad.4.m_ref = s32[8,128]{1,0:T(8,128)} pad(s32[8,32]{1,0:T(8,128)} %param.5, s32[]{:T(128)} %constant.2.clone.1), padding=0_0x0_96 | pad | bytes 5124 | tf_op jit(solution)/shard_map/jit(_pad)/pad | solution.py:287
  2.7 107.4 %shard_map.50 = (bf16[8,32,256]{2,1,0:T(8,128)(2,1)}, s32[8,8,128]{2,1,0:T(8,128)}) custom-call(bf16[8,32,3584]{2,1,0:T(8,128)(2,1)} %e_ref.1, bf16[448,3584]{1,0:T(8,128)(2,1)} %w_ref.1, s32[8,128]{1,0:T(8,128)} %pad.4.m_ref), custom_call_target="tpu_custom_call" | custom-call | tf_op jit(solution)/shard_map/pallas_call | solution.py:288
  110.1 0.9 convert_reduce_fusion
  111.0 0.8 convert_bitcast_fusion
  111.8 0.1 convert_element_type.25
  111.8 1.7 %fusion = (f32[8,32]{1,0:T(8,128)S(1)}, f32[8,32,256]{2,1,0:T(8,128)}) fusion(f32[8,256]{1,0:T(8,128)S(1)} %convert_element_type.25, f32[8,32]{1,0:T(8,128)S(1)} %convert_element_type.22, bf16[8,32,256]{2,1,0:T(8,128)(2,1)} %get-tuple-element.4), kind=kLoop, calls=%fused_computation.5 | loop fusion | flops 458496 | bytes 403456 | tf_op jit(solution)/shard_map/reduce_sum | solution.py:344
  113.6 0.0 copy-done
  113.6 0.7 multiply_divide_fusion
  (2 shorter events, 0.0 us)
Async XLA Ops:
  0.6 112.9 %copy-start = (s32[8,32]{1,0:T(8,128)S(1)}, s32[8,32]{1,0:T(8,128)}, u32[]{:S(2)}) copy-start(s32[8,32]{1,0:T(8,128)} %param.5) | copy-start | bytes 3076

commit v3 on v2

--- a/solution.py
+++ b/solution.py
@@ -47,8 +47,8 @@
     return lax.map(scores_of, pieces).reshape(prompts, block_rows, slots)
 
 
-def kernel(e_ref, w_ref, m_ref, s_ref, g_ref,
-           ebuf, wbuf, zbuf, sbuf, keep, pbuf, qbuf, fbuf, rbuf, mbuf,
+def kernel(e_ref, w_ref, m_ref, o_ref, r_ref,
+           ebuf, wbuf, zbuf, sbuf, keep, pbuf, qbuf, fbuf, rbuf, mine_cols, mbuf,
            m_send, m_recv, e_send, e_recv, ef_send, el_sem,
            w_send, w_recv, wl_sem, p_send, p_recv, f_send, r_recv):
     part = lax.axis_index("prompt")
@@ -80,6 +80,11 @@
     def arrived(dst, recv):
         copy(dst, dst, m_send.at[0], recv, z_far, core).wait_recv()
 
+    valid = m_ref[...].astype(jnp.float32)
+    slot = lax.broadcasted_iota(jnp.int32, (block_rows, rows), 1) - me * block_rows
+    place = (slot == lax.broadcasted_iota(jnp.int32, (block_rows, rows), 0)).astype(jnp.float32)
+    mine_cols[...] = jnp.dot(valid, place, preferred_element_type=jnp.float32).astype(jnp.int32)
+
     others = [lax.rem(me + d, group) for d in range(1, group)]
     plane = [lax.rem(part + d, PARTS) for d in range(1, PARTS)]
     barrier = pltpu.get_barrier_semaphore()
@@ -94,7 +99,7 @@
 
     def mask_copy(d):
         return pltpu.make_async_remote_copy(
-            m_ref, mbuf.at[me], m_send.at[d], m_recv.at[me],
+            mine_cols, mbuf.at[me], m_send.at[d], m_recv.at[me],
             device_id=(part, others[d]), device_id_type=MESH,
         )
 
@@ -103,10 +108,14 @@
     out_other = z_out * CORES + 1 - core - half * group // 2
     in_other = z_in * CORES + 1 - core - half * group // 2
     my_quarter = pl.multiple_of(part * quarter, 16)
-
-    def outer_w():
-        return copy(w_ref.at[pl.ds(my_quarter, quarter)], w_rows(my_block, my_quarter, quarter),
-                    w_send.at[0], w_recv.at[part], z_in, core)
+    first = quarter // 32 * 16
+    pieces = ((0, first), (first, quarter - first))
+
+    def outer_w(i):
+        at, size = pieces[i]
+        return copy(w_ref.at[pl.ds(pl.multiple_of(my_quarter + at, 16), size)],
+                    w_rows(my_block, my_quarter + at, size),
+                    w_send.at[0, i], w_recv.at[part, i], z_in, core)
 
     def outer_e(j, c):
         return copy(e_ref.at[c * per_core + j], ebuf.at[j, me],
@@ -128,18 +137,19 @@
         return copy(spot, spot, ef_send.at[j, c], e_recv.at[j, z_out * CORES + c], z_far, core)
 
     def near_w():
-        return copy(w_ref, w_rows(my_block, 0, held), w_send.at[0], w_recv.at[PARTS], z_in, 1 - core)
+        return copy(w_ref, w_rows(my_block, 0, held), w_send.at[0, 0], w_recv.at[PARTS, 0], z_in, 1 - core)
 
     def own_w():
         return pltpu.make_async_copy(w_ref, w_rows(my_block, 0, held), wl_sem.at[0])
 
-    def plane_w(d):
-        spot = w_rows(out_block, my_quarter, quarter)
-        return copy(spot, spot, w_send.at[1 + d], w_recv.at[part], z_in, core, plane[d])
+    def plane_w(d, i):
+        at, size = pieces[i]
+        spot = w_rows(out_block, my_quarter + at, size)
+        return copy(spot, spot, w_send.at[1 + d, i], w_recv.at[part, i], z_in, core, plane[d])
 
     def across_w():
         spot = w_rows(out_block, 0, held)
-        return copy(spot, spot, w_send.at[PARTS], w_recv.at[PARTS + 1], z_in, 1 - core)
+        return copy(spot, spot, w_send.at[PARTS, 0], w_recv.at[PARTS, 1], z_in, 1 - core)
 
     def partial_copy(j):
         return copy(pbuf.at[j], qbuf.at[j], p_send.at[j], p_recv.at[j], z_far, core)
@@ -155,7 +165,8 @@
 
     @pl.when(jnp.logical_not(inner))
     def _():
-        outer_w().start()
+        for i in range(2):
+            outer_w(i).start()
         for j in range(per_core):
             for c in range(CORES):
                 outer_e(j, c).start()
@@ -174,27 +185,31 @@
 
     for d in range(group - 1):
         mask_copy(d).start()
-    mbuf[me] = m_ref[...]
+    mbuf[me] = mine_cols[...]
 
     @pl.when(inner)
     def _():
-        arrived(w_rows(out_block, my_quarter, quarter), w_recv.at[part])
-        for d in range(PARTS - 1):
-            plane_w(d).start()
-
         def pass_on(j, carry):
             for c in range(CORES):
                 arrived(ebuf.at[j, z_out * CORES + c], e_recv.at[j, z_out * CORES + c])
                 onward_e(j, c).start()
             return carry
 
-        lax.fori_loop(0, per_core, pass_on, 0)
-        for q in plane:
-            arrived(w_rows(out_block, q * quarter, quarter), w_recv.at[q])
+        for i in range(2):
+            at, size = pieces[i]
+            arrived(w_rows(out_block, my_quarter + at, size), w_recv.at[part, i])
+            for d in range(PARTS - 1):
+                plane_w(d, i).start()
+        lax.fori_loop(0, per_core // 2, pass_on, 0)
+        for i in range(2):
+            at, size = pieces[i]
+            for q in plane:
+                arrived(w_rows(out_block, q * quarter + at, size), w_recv.at[q, i])
         across_w().start()
         own_w().wait()
-        arrived(w_rows(in_other, 0, held), w_recv.at[PARTS])
-        arrived(w_rows(out_other, 0, held), w_recv.at[PARTS + 1])
+        arrived(w_rows(in_other, 0, held), w_recv.at[PARTS, 0])
+        lax.fori_loop(per_core // 2, per_core - 1, pass_on, 0)
+        arrived(w_rows(out_other, 0, held), w_recv.at[PARTS, 1])
 
         mine_at = pl.multiple_of(half * half_rows, half_rows)
         theirs_at = pl.multiple_of((1 - half) * half_rows, half_rows)
@@ -208,24 +223,39 @@
             own_row = pl.multiple_of(my_block * block_rows, block_rows)
             rbuf[core * per_core + j] = fbuf[j, pl.ds(own_row, block_rows)]
 
-        def score(j, carry):
-            own_e(j).wait()
-            arrived(ebuf.at[j, z_in * CORES + 1 - core], e_recv.at[j, z_in * CORES + 1 - core])
-            for chip in (z_far, far_out):
-                for c in range(CORES):
-                    arrived(ebuf.at[j, chip * CORES + c], e_recv.at[j, chip * CORES + c])
-
-            def project(k, inside):
+        def project(j, block, blocks):
+            row = pl.multiple_of(block * block_rows, block_rows)
+
+            def chunk(k, inside):
                 start = pl.multiple_of(k * width, width)
-                left = ebuf[j].reshape(rows, features)
-                zbuf[:, pl.ds(start, width)] = lax.dot_general(
+                left = ebuf[j, pl.ds(block, blocks)].reshape(blocks * block_rows, features)
+                zbuf[j, pl.ds(row, blocks * block_rows), pl.ds(start, width)] = lax.dot_general(
                     left, wbuf[pl.ds(start, width)], NT, preferred_element_type=jnp.float32
                 ).astype(jnp.bfloat16)
                 return inside
 
-            lax.fori_loop(0, span // width, project, 0)
+            lax.fori_loop(0, span // width, chunk, 0)
+
+        def early(j, carry):
+            @pl.when(j == per_core - 2)
+            def _():
+                pass_on(per_core - 1, 0)
+
+            own_e(j).wait()
+            arrived(ebuf.at[j, z_in * CORES + 1 - core], e_recv.at[j, z_in * CORES + 1 - core])
+            for c in range(CORES):
+                arrived(ebuf.at[j, z_far * CORES + c], e_recv.at[j, z_far * CORES + c])
+            project(j, half * CORES, group - CORES)
+            return carry
+
+        lax.fori_loop(0, per_core, early, 0)
+
+        def score(j, carry):
+            for c in range(CORES):
+                arrived(ebuf.at[j, far_out * CORES + c], e_recv.at[j, far_out * CORES + c])
+            project(j, far_out * CORES, CORES)
             left = ebuf[j, :, :, lanes].reshape(rows, span)
-            right = zbuf[...]
+            right = zbuf[j]
             sbuf[...] = lax.dot_general(
                 left, right, NT, preferred_element_type=jnp.float32
             ) - lax.dot_general(right, left, NT, preferred_element_type=jnp.float32)
@@ -254,11 +284,13 @@
         near_w().wait_send()
         across_w().wait_send()
         for d in range(PARTS - 1):
-            plane_w(d).wait_send()
+            for i in range(2):
+                plane_w(d, i).wait_send()
 
     @pl.when(jnp.logical_not(inner))
     def _():
-        outer_w().wait_send()
+        for i in range(2):
+            outer_w(i).wait_send()
         for j in range(per_core):
             for c in range(CORES):
                 outer_e(j, c).wait_send()
@@ -268,8 +300,24 @@
     for d in range(group - 1):
         mask_copy(d).wait_send()
         arrived(mbuf.at[others[d]], m_recv.at[others[d]])
-    s_ref[...] = rbuf[...]
-    g_ref[...] = mbuf[...]
+    cols = mbuf[0]
+    for g in range(1, group):
+        cols = cols + mbuf[g]
+    cols = cols.astype(jnp.float32)
+    counts = jnp.sum(cols, axis=1, keepdims=True)
+    pairs = jnp.maximum(counts - 1.0, 1.0)
+    same = lax.broadcasted_iota(jnp.int32, (block_rows, block_rows), 0)
+    same = (same == lax.broadcasted_iota(jnp.int32, (block_rows, block_rows), 1)).astype(jnp.float32)
+    down = lax.dot_general(same, valid, NT, preferred_element_type=jnp.float32)
+    lane = lax.broadcasted_iota(jnp.int32, (block_rows, 128), 1)
+    rates = jnp.zeros((block_rows, 128), jnp.float32)
+    for p in range(prompts):
+        here = down[:, p:p + 1]
+        prefs = jax.nn.sigmoid(rbuf[p].astype(jnp.float32)) * here * cols[p:p + 1, :]
+        o_ref[p] = prefs
+        totals = jnp.sum(prefs, axis=1, keepdims=True) - 0.5 * here
+        rates = jnp.where(lane == p, here * totals / pairs[p:p + 1, :], rates)
+    r_ref[...] = jnp.transpose(rates)[:prompts]
 
 
 def line_scores(embeddings, head_weight, mask):
@@ -284,34 +332,34 @@
     dma = pltpu.SemaphoreType.DMA
     anywhere = pl.BlockSpec(memory_space=pl.ANY)
     vmem = pl.BlockSpec(memory_space=pltpu.VMEM)
-    padded = jnp.pad(mask, ((0, 0), (0, 128 - block_rows)))
     return pl.pallas_call(
         kernel,
         out_shape=(
-            jax.ShapeDtypeStruct((prompts, block_rows, rows), bf16),
-            jax.ShapeDtypeStruct((group, prompts, 128), jnp.int32),
+            jax.ShapeDtypeStruct((prompts, block_rows, rows), f32),
+            jax.ShapeDtypeStruct((prompts, block_rows), f32),
         ),
         in_specs=[anywhere, anywhere, vmem],
         out_specs=(vmem, vmem),
         scratch_shapes=[
             pltpu.VMEM((per_core, group, block_rows, features), bf16),
             pltpu.VMEM((span, features), bf16),
-            pltpu.VMEM((rows, span), bf16),
+            pltpu.VMEM((per_core, rows, span), bf16),
             pltpu.VMEM((rows, rows), f32),
             pltpu.VMEM((per_core, half_rows, rows), f32),
             pltpu.VMEM((per_core, half_rows, rows), bf16),
             pltpu.VMEM((per_core, half_rows, rows), bf16),
             pltpu.VMEM((per_core, half_rows, rows), bf16),
             pltpu.VMEM((prompts, block_rows, rows), bf16),
-            pltpu.VMEM((group, prompts, 128), jnp.int32),
+            pltpu.VMEM((prompts, rows), jnp.int32),
+            pltpu.VMEM((group, prompts, rows), jnp.int32),
             dma((group - 1,)),
             dma((group,)),
             dma((per_core, 3)),
             dma((per_core, group)),
             dma((per_core, CORES)),
             dma((per_core,)),
-            dma((PARTS + 1,)),
-            dma((PARTS + 2,)),
+            dma((PARTS + 1, 2)),
+            dma((PARTS + 1, 2)),
             dma((1,)),
             dma((per_core,)),
             dma((per_core,)),
@@ -321,25 +369,19 @@
         compiler_params=pltpu.CompilerParams(
             collective_id=0, has_side_effects=True, vmem_limit_bytes=56 << 20
         ),
-    )(embeddings, head_weight, padded)
+    )(embeddings, head_weight, mask)
 
 
 def shards(embeddings, head_weight, valid_mask):
     group_size = lax.axis_size("resp")
-    prompts, block_rows, features = embeddings.shape
-    slots = group_size * block_rows
+    slots = group_size * embeddings.shape[1]
+    if (lax.axis_size("prompt"), group_size) == (PARTS, CHIPS * CORES):
+        return line_scores(embeddings, head_weight, valid_mask)
     valid_rows = valid_mask.astype(jnp.float32)
-    if (lax.axis_size("prompt"), group_size) == (PARTS, CHIPS * CORES):
-        scores, masks = line_scores(embeddings, head_weight, valid_mask)
-        scores = scores.astype(jnp.float32)
-        valid_cols = jnp.transpose(masks[:, :, :block_rows], (1, 0, 2)).reshape(prompts, slots)
-        valid_cols = valid_cols.astype(jnp.float32)
-        counts = jnp.sum(valid_cols, axis=1)
-    else:
-        counts = lax.psum(jnp.sum(valid_rows, axis=1), "resp")
-        scores = gathered_scores(embeddings, head_weight)
-        column_ids = jnp.arange(slots, dtype=jnp.float32)
-        valid_cols = (column_ids[None, :] < counts[:, None]).astype(jnp.float32)
+    counts = lax.psum(jnp.sum(valid_rows, axis=1), "resp")
+    scores = gathered_scores(embeddings, head_weight)
+    column_ids = jnp.arange(slots, dtype=jnp.float32)
+    valid_cols = (column_ids[None, :] < counts[:, None]).astype(jnp.float32)
     preferences = jax.nn.sigmoid(scores) * valid_rows[:, :, None] * valid_cols[:, None, :]
     totals = jnp.sum(preferences, axis=2) - 0.5 * valid_rows
     win_rates = valid_rows * totals / jnp.maximum(counts - 1.0, 1.0)[:, None]

time: 115 us -> 112 us (0.974)
  other arithmetic: 4.78 us -> 0 us
  local copies, waits for them, and re-layouts: 1.38 us -> 2.95 us
    unnamed x2, local copies, waits for them, and re-layouts: 0.01 us -> 2.95 us
    reduce_sum x2 -> x0, other arithmetic: 2.59 us -> none  [the longest x1 1.71 us: shards(): totals = jnp.sum(preferences, axis=2) - 0.5 * valid_rows]
    convert_element_type x2 -> x0, other arithmetic: 1.52 us -> none  [the longest x1 0.76 us: shards(): valid_cols = valid_cols.astype(jnp.float32)]
    pad x1 -> x0, local copies, waits for them, and re-layouts: 1.28 us -> none  [line_scores(): padded = jnp.pad(mask, ((0, 0), (0, 128 - block_rows)))]
where the time goes in v3:
time: 112 us
  Pallas kernels  108 us (96%)
  local copies, waits for them, and re-layouts  2.95 us (3%)
    pallas_call x1, Pallas kernels, line_scores(): pl.pallas_call(kernel, out_shape=(jax.ShapeDtypeStruct((prompts, block_ro...  108 us
    unnamed x2, local copies, waits for them, and re-layouts  2.95 us

profile of v3, /device:TPU:0, one launch (start us, length us, event | category | flops | bytes accessed | tf_op | source)
XLA Modules:
  0.0 111.7 jit_solution(8629498088402502798)
XLA Ops:
  0.6 108.2 %shard_map.50 = (f32[8,32,256]{2,1,0:T(8,128)}, f32[8,32]{1,0:T(8,128)}) custom-call(bf16[8,32,3584]{2,1,0:T(8,128)(2,1)} %e_ref.1, bf16[448,3584]{1,0:T(8,128)(2,1)} %w_ref.1, s32[8,32]{1,0:T(8,128)} %m_ref.1), custom_call_target="tpu_custom_call" | custom-call | tf_op jit(solution)/shard_map/pallas_call | solution.py:335
  108.8 1.7 %copy.7 = f32[8,32,256]{2,1,0:T(8,128)} copy(f32[8,32,256]{2,1,0:T(8,128)} %get-tuple-element.4) | data formatting | bytes 524288
  110.5 1.3 %copy.8 = f32[8,32]{1,0:T(8,128)} copy(f32[8,32]{1,0:T(8,128)} %get-tuple-element.5) | data formatting | bytes 2048

commit v4 on v3

--- a/solution.py
+++ b/solution.py
@@ -50,7 +50,7 @@
 def kernel(e_ref, w_ref, m_ref, o_ref, r_ref,
            ebuf, wbuf, zbuf, sbuf, keep, pbuf, qbuf, fbuf, rbuf, mine_cols, mbuf,
            m_send, m_recv, e_send, e_recv, ef_send, el_sem,
-           w_send, w_recv, wl_sem, p_send, p_recv, f_send, r_recv):
+           w_send, w_recv, a_send, a_recv, wl_sem, p_send, p_recv, f_send, r_recv):
     part = lax.axis_index("prompt")
     me = lax.axis_index("resp")
     z = me // CORES
@@ -147,9 +147,10 @@
         spot = w_rows(out_block, my_quarter + at, size)
         return copy(spot, spot, w_send.at[1 + d, i], w_recv.at[part, i], z_in, core, plane[d])
 
-    def across_w():
-        spot = w_rows(out_block, 0, held)
-        return copy(spot, spot, w_send.at[PARTS, 0], w_recv.at[PARTS, 1], z_in, 1 - core)
+    def across_w(q, i):
+        at, size = pieces[i]
+        spot = w_rows(out_block, q * quarter + at, size)
+        return copy(spot, spot, a_send.at[q, i], a_recv.at[q, i], z_in, 1 - core)
 
     def partial_copy(j):
         return copy(pbuf.at[j], qbuf.at[j], p_send.at[j], p_recv.at[j], z_far, core)
@@ -200,16 +201,20 @@
             arrived(w_rows(out_block, my_quarter + at, size), w_recv.at[part, i])
             for d in range(PARTS - 1):
                 plane_w(d, i).start()
+            across_w(part, i).start()
         lax.fori_loop(0, per_core // 2, pass_on, 0)
         for i in range(2):
             at, size = pieces[i]
             for q in plane:
                 arrived(w_rows(out_block, q * quarter + at, size), w_recv.at[q, i])
-        across_w().start()
+                across_w(q, i).start()
         own_w().wait()
         arrived(w_rows(in_other, 0, held), w_recv.at[PARTS, 0])
         lax.fori_loop(per_core // 2, per_core - 1, pass_on, 0)
-        arrived(w_rows(out_other, 0, held), w_recv.at[PARTS, 1])
+        for i in range(2):
+            at, size = pieces[i]
+            for q in range(PARTS):
+                arrived(w_rows(out_other, q * quarter + at, size), a_recv.at[q, i])
 
         mine_at = pl.multiple_of(half * half_rows, half_rows)
         theirs_at = pl.multiple_of((1 - half) * half_rows, half_rows)
@@ -223,37 +228,52 @@
             own_row = pl.multiple_of(my_block * block_rows, block_rows)
             rbuf[core * per_core + j] = fbuf[j, pl.ds(own_row, block_rows)]
 
-        def project(j, block, blocks):
+        def project(j, many, block, blocks):
             row = pl.multiple_of(block * block_rows, block_rows)
+            tall = blocks * block_rows
 
             def chunk(k, inside):
                 start = pl.multiple_of(k * width, width)
-                left = ebuf[j, pl.ds(block, blocks)].reshape(blocks * block_rows, features)
-                zbuf[j, pl.ds(row, blocks * block_rows), pl.ds(start, width)] = lax.dot_general(
+                left = ebuf[pl.ds(j, many), pl.ds(block, blocks)].reshape(many * tall, features)
+                zbuf[pl.ds(j, many), pl.ds(row, tall), pl.ds(start, width)] = lax.dot_general(
                     left, wbuf[pl.ds(start, width)], NT, preferred_element_type=jnp.float32
-                ).astype(jnp.bfloat16)
+                ).astype(jnp.bfloat16).reshape(many, tall, width)
                 return inside
 
             lax.fori_loop(0, span // width, chunk, 0)
 
-        def early(j, carry):
-            @pl.when(j == per_core - 2)
+        pair = per_core // 2
+
+        def early(n, carry):
+            @pl.when(n == 1)
             def _():
                 pass_on(per_core - 1, 0)
 
-            own_e(j).wait()
-            arrived(ebuf.at[j, z_in * CORES + 1 - core], e_recv.at[j, z_in * CORES + 1 - core])
-            for c in range(CORES):
-                arrived(ebuf.at[j, z_far * CORES + c], e_recv.at[j, z_far * CORES + c])
-            project(j, half * CORES, group - CORES)
+            for i in range(pair):
+                j = n * pair + i
+                own_e(j).wait()
+                arrived(ebuf.at[j, z_in * CORES + 1 - core], e_recv.at[j, z_in * CORES + 1 - core])
+                for c in range(CORES):
+                    arrived(ebuf.at[j, z_far * CORES + c], e_recv.at[j, z_far * CORES + c])
+            project(n * pair, pair, half * CORES, group - CORES)
             return carry
 
-        lax.fori_loop(0, per_core, early, 0)
+        lax.fori_loop(0, 2, early, 0)
+
+        def last_rows(j, carry):
+            for c in range(CORES):
+                arrived(ebuf.at[j, far_out * CORES + c], e_recv.at[j, far_out * CORES + c])
+            return carry
+
+        lax.fori_loop(0, per_core - 1, last_rows, 0)
+        project(0, per_core - 1, far_out * CORES, CORES)
 
         def score(j, carry):
-            for c in range(CORES):
-                arrived(ebuf.at[j, far_out * CORES + c], e_recv.at[j, far_out * CORES + c])
-            project(j, far_out * CORES, CORES)
+            @pl.when(j == per_core - 1)
+            def _():
+                last_rows(per_core - 1, 0)
+                project(per_core - 1, 1, far_out * CORES, CORES)
+
             left = ebuf[j, :, :, lanes].reshape(rows, span)
             right = zbuf[j]
             sbuf[...] = lax.dot_general(
@@ -282,7 +302,9 @@
             for t in range(group // 2 - 1):
                 final_copy(j, t).wait_send()
         near_w().wait_send()
-        across_w().wait_send()
+        for i in range(2):
+            for q in range(PARTS):
+                across_w(q, i).wait_send()
         for d in range(PARTS - 1):
             for i in range(2):
                 plane_w(d, i).wait_send()
@@ -358,8 +380,10 @@
             dma((per_core, group)),
             dma((per_core, CORES)),
             dma((per_core,)),
-            dma((PARTS + 1, 2)),
-            dma((PARTS + 1, 2)),
+            dma((PARTS, 2)),
+            dma((PARTS + 1, 1 + 1)),
+            dma((PARTS, 2)),
+            dma((PARTS, 2)),
             dma((1,)),
             dma((per_core,)),
             dma((per_core,)),

time: 112 us -> 108 us (0.964)
  Pallas kernels: 108 us -> 104 us
    pallas_call x1, Pallas kernels: 108 us -> 104 us  [line_scores(): pl.pallas_call(kernel, out_shape=(jax.ShapeDtypeStruct((prompts, block_ro...]
where the time goes in v4:
time: 108 us
  Pallas kernels  104 us (96%)
  local copies, waits for them, and re-layouts  2.95 us (3%)
    pallas_call x1, Pallas kernels, line_scores(): pl.pallas_call(kernel, out_shape=(jax.ShapeDtypeStruct((prompts, block_ro...  104 us
    unnamed x2, local copies, waits for them, and re-layouts  2.95 us

profile of v4, /device:TPU:0, one launch (start us, length us, event | category | flops | bytes accessed | tf_op | source)
XLA Modules:
  0.0 107.8 jit_solution(783076541185722502)
XLA Ops:
  0.6 104.2 %shard_map.50 = (f32[8,32,256]{2,1,0:T(8,128)}, f32[8,32]{1,0:T(8,128)}) custom-call(bf16[8,32,3584]{2,1,0:T(8,128)(2,1)} %e_ref.1, bf16[448,3584]{1,0:T(8,128)(2,1)} %w_ref.1, s32[8,32]{1,0:T(8,128)} %m_ref.1), custom_call_target="tpu_custom_call" | custom-call | tf_op jit(solution)/shard_map/pallas_call | solution.py:357
  104.9 1.7 %copy.7 = f32[8,32,256]{2,1,0:T(8,128)} copy(f32[8,32,256]{2,1,0:T(8,128)} %get-tuple-element.4) | data formatting | bytes 524288
  106.6 1.3 %copy.8 = f32[8,32]{1,0:T(8,128)} copy(f32[8,32]{1,0:T(8,128)} %get-tuple-element.5) | data formatting | bytes 2048

commit v5 on v4

--- a/solution.py
+++ b/solution.py
@@ -282,15 +282,11 @@
             pbuf[j] = sbuf[pl.ds(theirs_at, half_rows)].astype(jnp.bfloat16)
             partial_copy(j).start()
             keep[j] = sbuf[pl.ds(mine_at, half_rows)]
-
-            @pl.when(j > 0)
-            def _():
-                finish(j - 1)
-
             return carry
 
         lax.fori_loop(0, per_core, score, 0)
-        finish(per_core - 1)
+        for j in range(per_core):
+            finish(j)
         for j in range(per_core):
             arrived(rbuf.at[(1 - core) * per_core + j], r_recv.at[(1 - core) * per_core + j])
         for j in range(per_core):

time: 108 us -> 106 us (0.981)
  Pallas kernels: 104 us -> 102 us
    pallas_call x1, Pallas kernels: 104 us -> 102 us  [line_scores(): pl.pallas_call(kernel, out_shape=(jax.ShapeDtypeStruct((prompts, block_ro...]
where the time goes in v5:
time: 106 us
  Pallas kernels  102 us (96%)
  local copies, waits for them, and re-layouts  2.95 us (3%)
    pallas_call x1, Pallas kernels, line_scores(): pl.pallas_call(kernel, out_shape=(jax.ShapeDtypeStruct((prompts, block_ro...  102 us
    unnamed x2, local copies, waits for them, and re-layouts  2.95 us

profile of v5, /device:TPU:0, one launch (start us, length us, event | category | flops | bytes accessed | tf_op | source)
XLA Modules:
  0.0 105.5 jit_solution(12897419995467779145)
XLA Ops:
  0.6 102.0 %shard_map.50 = (f32[8,32,256]{2,1,0:T(8,128)}, f32[8,32]{1,0:T(8,128)}) custom-call(bf16[8,32,3584]{2,1,0:T(8,128)(2,1)} %e_ref.1, bf16[448,3584]{1,0:T(8,128)(2,1)} %w_ref.1, s32[8,32]{1,0:T(8,128)} %m_ref.1), custom_call_target="tpu_custom_call" | custom-call | tf_op jit(solution)/shard_map/pallas_call | solution.py:353
  102.6 1.7 %copy.7 = f32[8,32,256]{2,1,0:T(8,128)} copy(f32[8,32,256]{2,1,0:T(8,128)} %get-tuple-element.4) | data formatting | bytes 524288
  104.3 1.3 %copy.8 = f32[8,32]{1,0:T(8,128)} copy(f32[8,32]{1,0:T(8,128)} %get-tuple-element.5) | data formatting | bytes 2048
